TPU v7x, 32 devices: a whole 2x2x4 slice. The times are simulated.
32 devices in a mesh: depth: 8 (over z, core), gx: 4 (over y, x).
Axes of the slice: x: 2, y: 2, z: 4, core: 2. Of those that a mesh axis runs over, the one named last changes fastest.
Arguments:
- pressure_now: float32 [4, 128, 256, 128], P(None, 'gx', 'depth'), may hold values from -6 to 6
- pressure_before: float32 [4, 128, 256, 128], P(None, 'gx', 'depth'), may hold values from -6 to 6
- class_map: int32 [128, 256, 128], P('gx', 'depth'), may hold values from 0 to 7
- courant_sq: float32 [8], replicated, may hold values from 0.02 to 0.12
- source_cells: int32 [4, 3], replicated, may hold values from 0 to 255, as said below
- source_wavelet: float32 [8, 4], replicated, may hold values from -6 to 6
- layer_start: int32 [1], replicated, may hold values from 232 to 240
Outputs:
- pressure_final: float32 [4, 128, 256, 128], P(None, 'gx', 'depth')
- pressure_prior: float32 [4, 128, 256, 128], P(None, 'gx', 'depth')
Inputs may be any that keep to these rules, and one draw needn't show every extreme that they name: `source_cells`: each row holds a cell inside the grid: x below 128, depth below 256, y below 128; shot 0 sits at the last cell along every dimension and shot 1 at cell (0, 0, 0).
All inputs are finite; a program needn't handle non-finite values.
Results may differ from a plain program's by a relative error of at most 0.00002.
Values sent between devices are 32-bit elements; how exact they have to be, the bound alone decides.
A program may use at most 128 MiB of HBM per device.

v0:
```python
import functools
import math

import jax
import jax.numpy as jnp
from jax import lax
from jax.experimental import pallas as pl
from jax.experimental.pallas import tpu as pltpu
from jax.sharding import PartitionSpec as P

COEFFS = (-205.0 / 72.0, 8.0 / 5.0, -1.0 / 5.0, 8.0 / 315.0, -1.0 / 560.0)
DAMPING = 0.3
GROUP = 8
W = 4
T = 8
DIRS = (("depth", -1), ("depth", 1), ("gx", -1), ("gx", 1))


def kernel(
    sizes, iters, shots, rows, depth, width, classes,
    now_hbm, before_hbm, class_hbm, courant, cells, wavelet, start,
    final_hbm, prior_hbm,
    grid, speed, scale, klass, load_sem, class_sem, out_sem, send_sem, recv_sem,
):
    place = {axis: lax.axis_index(axis) for axis in ("depth", "gx")}
    has = []
    for axis, delta in DIRS:
        has.append(place[axis] > 0 if delta < 0 else place[axis] < sizes[axis] - 1)

    def target(d):
        axis, delta = DIRS[d]
        there = dict(place)
        there[axis] = place[axis] + delta
        return (there["depth"], there["gx"])

    xs, zs = pl.ds(W, rows), pl.ds(T, depth)

    def load(source, buf, s, k):
        return pltpu.make_async_copy(
            source.at[s], grid.at[buf, s, xs, zs, :], load_sem.at[k, s]
        )

    for s in range(shots):
        load(now_hbm, 0, s, 0).start()
    load_class = pltpu.make_async_copy(class_hbm, klass, class_sem)
    load_class.start()
    for s in range(shots):
        load(before_hbm, 1, s, 1).start()

    faces = (
        ((xs, pl.ds(T, T)), (xs, pl.ds(T + depth, T))),
        ((xs, pl.ds(depth, T)), (xs, pl.ds(0, T))),
        ((pl.ds(W, W), zs), (pl.ds(W + rows, W), zs)),
        ((pl.ds(rows, W), zs), (pl.ds(0, W), zs)),
    )

    def halo(buf, s, d):
        (sx, sz), (dx, dz) = faces[d]
        return pltpu.make_async_remote_copy(
            src_ref=grid.at[buf, s, sx, sz, :],
            dst_ref=grid.at[buf, s, dx, dz, :],
            send_sem=send_sem.at[buf, s, d],
            recv_sem=recv_sem.at[buf, s, d],
            device_id=target(d),
            device_id_type=pl.DeviceIdType.MESH,
        )

    for d in range(4):
        dx, dz = faces[d ^ 1][1]

        @pl.when(jnp.logical_not(has[d]))
        def _():
            for buf in range(2):
                def clear(s, c):
                    shape = (dx.size, dz.size, width)
                    grid[buf, s, dx, dz, :] = jnp.zeros(shape, jnp.float32)
                    return c
                lax.fori_loop(0, shots, clear, 0)

    barrier = pltpu.get_barrier_semaphore()
    for d in range(4):
        @pl.when(has[d])
        def _():
            pl.semaphore_signal(
                barrier, inc=1, device_id=target(d), device_id_type=pl.DeviceIdType.MESH
            )
    peers = sum(present.astype(jnp.int32) for present in has)
    pl.semaphore_wait(barrier, peers)

    def send(buf, s, ways=(2, 3, 0, 1)):
        for d in ways:
            @pl.when(has[d])
            def _():
                halo(buf, s, d).start()

    for s in range(shots):
        load(now_hbm, 0, s, 0).wait()
        send(0, s)

    z_index = place["depth"] * depth + lax.broadcasted_iota(jnp.int32, (depth, width), 0)
    total = depth * sizes["depth"]
    begin = jnp.full((depth, width), start[0], jnp.int32)
    ratio = (z_index - begin + 1).astype(jnp.float32) / (total - begin).astype(jnp.float32)
    damping = jnp.where(z_index >= begin, DAMPING * ratio * ratio, jnp.float32(0.0))
    inverse = 1.0 / (1.0 + damping)
    scale[0] = inverse
    scale[1] = 2.0 * inverse

    load_class.wait()

    def lookup(x, c):
        held = klass[x]
        value = jnp.zeros((depth, width), jnp.float32)
        for k in range(classes):
            value = jnp.where(held == k, courant[k], value)
        speed[x] = value * scale[0]
        return c

    lax.fori_loop(0, rows, lookup, 0)
    for s in range(shots):
        load(before_hbm, 1, s, 1).wait()

    lane = lax.broadcasted_iota(jnp.int32, (T, width), 1)
    low = [jnp.where(lane >= k, jnp.float32(COEFFS[k]), 0.0) for k in range(1, W + 1)]
    high = [jnp.where(lane < width - k, jnp.float32(COEFFS[k]), 0.0) for k in range(1, W + 1)]
    x_anchor = place["gx"] * rows

    def compute(t, s, buf, other):
        lane_z = lax.broadcasted_iota(jnp.int32, (depth, width), 1)
        hit = (z_index == cells[s, 1]) & (lane_z == cells[s, 2])
        pulse = jnp.where(hit, wavelet[t, s] * scale[0], 0.0)
        cell_x = cells[s, 0] - x_anchor

        group = math.gcd(rows, GROUP)

        def block_of(x, j):
            z = T + j * T

            def at(dx, dz):
                return grid[buf, s, x + W + dx, pl.ds(z + dz, T), :]

            p = at(0, 0)
            lap = (3.0 * COEFFS[0]) * p
            for k in range(1, W + 1):
                pair = (at(k, 0) + at(-k, 0)) + (at(0, k) + at(0, -k))
                lap = lap + COEFFS[k] * pair
                lap = lap + (
                    low[k - 1] * pltpu.roll(p, k, 1)
                    + high[k - 1] * pltpu.roll(p, width - k, 1)
                )
            q = grid[other, s, x + W, pl.ds(z, T), :]
            block = pl.ds(j * T, T)
            nxt = scale[1, block, :] * (p - q) + q + speed[x, block, :] * lap
            amp = jnp.where(x == cell_x, jnp.float32(1.0), jnp.float32(0.0))
            return nxt + amp * pulse[j * T : (j + 1) * T]

        def row(g, c):
            spots = [(g * group + i, j) for i in range(group) for j in range(depth // T)]
            values = [block_of(x, j) for x, j in spots]
            for (x, j), value in zip(spots, values):
                grid[other, s, x + W, pl.ds(T + j * T, T), :] = value
            return c

        count = rows // group
        edges = min(count, 2)
        lax.fori_loop(0, edges, lambda g, c: row(g * (count - 1), c), 0)

        @pl.when(t < iters - 1)
        def _():
            send(other, s, (2, 3))

        lax.fori_loop(1, count - 1, row, 0)

    def store(buf, s, out, k):
        return pltpu.make_async_copy(grid.at[buf, s, xs, zs, :], out.at[s], out_sem.at[k, s])

    def step(t, c):
        buf = lax.rem(t, 2)
        other = 1 - buf

        def shot(s, c):
            for d in range(4):
                @pl.when(has[d ^ 1])
                def _():
                    halo(buf, s, d).wait_recv()

            @pl.when(t >= 1)
            def _():
                for d in range(4):
                    @pl.when(has[d])
                    def _():
                        halo(other, s, d).wait_send()

            compute(t, s, buf, other)

            @pl.when(t < iters - 1)
            def _():
                send(other, s, (0, 1))

            @pl.when(t == iters - 1)
            def _():
                store(iters % 2, s, final_hbm, 0).start()
                store(1 - iters % 2, s, prior_hbm, 1).start()

            return c

        return lax.fori_loop(0, shots, shot, c)

    lax.fori_loop(0, iters, step, 0)
    for s in range(shots):
        for d in range(4):
            @pl.when(has[d])
            def _():
                halo(1 - iters % 2, s, d).wait_send()
        store(iters % 2, s, final_hbm, 0).wait()
        store(1 - iters % 2, s, prior_hbm, 1).wait()


def solution(mesh):
    sizes = {axis: mesh.shape[axis] for axis in ("depth", "gx")}

    def local(now, before, class_map, courant, cells, wavelet, start):
        shots, rows, depth, width = now.shape
        iters = wavelet.shape[0]
        body = functools.partial(
            kernel, sizes, iters, shots, rows, depth, width, courant.shape[0]
        )
        whole = pl.BlockSpec(memory_space=pl.ANY)
        scalar = pl.BlockSpec(memory_space=pltpu.SMEM)
        out = jax.ShapeDtypeStruct(now.shape, jnp.float32)
        return pl.pallas_call(
            body,
            out_shape=(out, out),
            in_specs=[whole] * 3 + [scalar] * 4,
            out_specs=(whole, whole),
            scratch_shapes=[
                pltpu.VMEM((2, shots, rows + 2 * W, depth + 2 * T, width), jnp.float32),
                pltpu.VMEM((rows, depth, width), jnp.float32),
                pltpu.VMEM((2, depth, width), jnp.float32),
                pltpu.VMEM((rows, depth, width), jnp.int32),
                pltpu.SemaphoreType.DMA((2, shots)),
                pltpu.SemaphoreType.DMA,
                pltpu.SemaphoreType.DMA((2, shots)),
                pltpu.SemaphoreType.DMA((2, shots, 4)),
                pltpu.SemaphoreType.DMA((2, shots, 4)),
            ],
            compiler_params=pltpu.CompilerParams(collective_id=0, has_side_effects=True),
            name="wave",
        )(now, before, class_map, courant, cells, wavelet, start)

    placed = P(None, "gx", "depth", None)
    return jax.shard_map(
        local,
        mesh=mesh,
        in_specs=(placed, placed, P("gx", "depth", None), P(), P(), P(), P()),
        out_specs=(placed, placed),
        check_vma=False,
    )
```

profile of v0, /device:TPU:0, one launch (start us, length us, event | category | flops | bytes accessed | tf_op | source)
XLA Modules:
  0.0 105.7 jit_solution(14977356757243087392)
XLA Ops:
  1.3 1.3 %copy.9.wavelet = f32[8,4]{1,0:T(8,128)} copy(f32[8,4]{0,1:T(4,128)} %param.12) | data formatting | bytes 256 | tf_op args[5]
  2.6 98.5 %wave.1 = (f32[4,32,32,128]{3,2,1,0:T(8,128)}, f32[4,32,32,128]{3,2,1,0:T(8,128)}) custom-call(f32[4,32,32,128]{3,2,1,0:T(8,128)} %now_hbm.1, f32[4,32,32,128]{3,2,1,0:T(8,128)} %before_hbm.1, s32[32,32,128]{2,1,0:T(8,128)} %class_hbm.1, f32[8]{0:T(128)} %courant.1, s32[4,3]{1,0:T(4,128)} %cells.1, f32[8,4]{1,0:T(8,128)} %copy.9.wavelet, s32[1]{0:T(128)S(6)} %copy.12.start), custom_call_target="tpu_custom_call" | custom-call | tf_op jit(solution)/shard_map/wave/pallas_call | solution.py:231
  101.1 0.0 copy-start
  101.2 3.2 %copy.13 = f32[4,32,32,128]{3,2,1,0:T(8,128)} copy(f32[4,32,32,128]{3,2,1,0:T(8,128)} %get-tuple-element.4) | data formatting | bytes 4194304
  104.4 0.0 copy-done
  104.4 1.3 %copy.14 = f32[4,32,32,128]{3,2,1,0:T(8,128)} copy(f32[4,32,32,128]{3,2,1,0:T(8,128)S(1)} %copy-done) | data formatting | bytes 4194304
Async XLA Ops:
  101.1 3.2 %copy-start = (f32[4,32,32,128]{3,2,1,0:T(8,128)S(1)}, f32[4,32,32,128]{3,2,1,0:T(8,128)}, u32[]{:S(2)}) copy-start(f32[4,32,32,128]{3,2,1,0:T(8,128)} %get-tuple-element.5) | copy-start | bytes 6291460
where the time goes:
time: 106 us
  Pallas kernels  98.5 us (93%)
  local copies, waits for them, and re-layouts  5.9 us (6%)
  between operations  1.29 us (1%)
    pallas_call x1, Pallas kernels, local(): pl.pallas_call(body, out_shape=(out, out), in_specs=[whole] * 3 + [scalar...  98.5 us
    unnamed x5, local copies, waits for them, and re-layouts  5.9 us

commit v1 on v0

v1 whole, which is shorter than its diff:
```python
import functools
import math

import jax
import jax.numpy as jnp
from jax import lax
from jax.experimental import pallas as pl
from jax.experimental.pallas import tpu as pltpu
from jax.sharding import PartitionSpec as P

COEFFS = (-205.0 / 72.0, 8.0 / 5.0, -1.0 / 5.0, 8.0 / 315.0, -1.0 / 560.0)
DAMPING = 0.3
GROUP = 8
W = 4
T = 8
LAG = 1
DIRS = (("depth", -1), ("depth", 1), ("gx", -1), ("gx", 1))
MESH = pl.DeviceIdType.MESH


def kernel(
    sizes, side, iters, shots, rows, depth, width, classes,
    now_hbm, before_hbm, class_hbm, courant, cells, wavelet, start,
    grid,
    relay, speed, scale, klass, load_sem, class_sem,
    send_sem, recv_sem, relay_sem, forward_sem,
):
    place = {axis: lax.axis_index(axis) for axis in ("depth", "gx")}
    me = place["gx"]
    lanes = sizes["gx"]
    has = []
    for axis, delta in DIRS:
        has.append(place[axis] > 0 if delta < 0 else place[axis] < sizes[axis] - 1)

    def along(g):
        return (place["depth"], g)

    def target(d):
        axis, delta = DIRS[d]
        there = dict(place)
        there[axis] = place[axis] + delta
        return (there["depth"], there["gx"])

    relayed = side > 1
    if relayed:
        column = lax.rem(me, side)
        cross = {2: has[2] & (column == 0), 3: has[3] & (column == side - 1)}
        via = {2: me - side, 3: me + side}
        serves = {
            2: (column == 0) & (me + side < lanes),
            3: (column == side - 1) & (me - side >= 0),
        }
        serve_from = {2: me + side, 3: me - side}
        serve_to = {2: me + side - 1, 3: me - side + 1}

    half = max(T, depth // 2 // T * T) if relayed else depth

    xs, zs = pl.ds(W, rows), pl.ds(T, depth)
    za, zb = pl.ds(T, half), pl.ds(T + half, depth - half)

    def load(source, buf, s, k):
        return pltpu.make_async_copy(
            source.at[s], grid.at[buf, s, xs, zs, :], load_sem.at[k, s]
        )

    for s in range(shots):
        load(now_hbm, 0, s, 0).start()
    load_class = pltpu.make_async_copy(class_hbm, klass, class_sem)
    load_class.start()
    for s in range(shots):
        load(before_hbm, 1, s, 1).start()

    pieces = [
        (0, xs, pl.ds(T, T), xs, pl.ds(T + depth, T)),
        (1, xs, pl.ds(depth, T), xs, pl.ds(0, T)),
        (2, pl.ds(W, W), za, pl.ds(W + rows, W), za),
        (3, pl.ds(rows, W), za, pl.ds(0, W), za),
    ]
    if relayed:
        pieces += [
            (2, pl.ds(W, W), zb, pl.ds(W + rows, W), zb),
            (3, pl.ds(rows, W), zb, pl.ds(0, W), zb),
        ]

    def halo(buf, s, k):
        d, sx, sz, dx, dz = pieces[k]
        return pltpu.make_async_remote_copy(
            src_ref=grid.at[buf, s, sx, sz, :],
            dst_ref=grid.at[buf, s, dx, dz, :],
            send_sem=send_sem.at[buf, s, k],
            recv_sem=recv_sem.at[buf, s, k],
            device_id=target(d),
            device_id_type=MESH,
        )

    def detour(r, buf, s, k):
        d, sx, sz, _, _ = pieces[k]
        return pltpu.make_async_remote_copy(
            src_ref=grid.at[buf, s, sx, sz, :],
            dst_ref=relay.at[r, s],
            send_sem=send_sem.at[buf, s, k],
            recv_sem=relay_sem.at[r, s],
            device_id=along(via[d]),
            device_id_type=MESH,
        )

    def forward(r, buf, s, k):
        d, _, _, dx, dz = pieces[k]
        return pltpu.make_async_remote_copy(
            src_ref=relay.at[r, s],
            dst_ref=grid.at[buf, s, dx, dz, :],
            send_sem=forward_sem.at[r, s],
            recv_sem=recv_sem.at[buf, s, k],
            device_id=along(serve_to[d]),
            device_id_type=MESH,
        )

    for d in range(4):
        _, _, _, dx, dz = pieces[d ^ 1]
        if d >= 2:
            dz = zs

        @pl.when(jnp.logical_not(has[d]))
        def _():
            for buf in range(2):
                def clear(s, c):
                    shape = (dx.size, dz.size, width)
                    grid[buf, s, dx, dz, :] = jnp.zeros(shape, jnp.float32)
                    return c
                lax.fori_loop(0, shots, clear, 0)

    meets = [(has[d], target(d)) for d in range(4)]
    if relayed:
        for d in (2, 3):
            step_back = -side + 1 if d == 2 else side - 1
            back = me - step_back - (1 if d == 2 else -1)
            meets.append((cross[d], along(via[d])))
            meets.append((serves[d], along(serve_from[d])))
            if side > 2:
                meets.append((serves[d], along(serve_to[d])))
                meets.append((cross[d], along(me + (side - 1 if d == 2 else 1 - side))))

    barrier = pltpu.get_barrier_semaphore()
    for there, device in meets:
        @pl.when(there)
        def _():
            pl.semaphore_signal(barrier, inc=1, device_id=device, device_id_type=MESH)
    peers = sum(there.astype(jnp.int32) for there, _ in meets)
    pl.semaphore_wait(barrier, peers)

    def each(ways, straight, around):
        for k in ways:
            d = pieces[k][0]
            if k < 4:
                pl.when(has[d])(lambda: straight(k))
            else:
                pl.when(cross[d])(lambda: around(k))
                pl.when(has[d] & jnp.logical_not(cross[d]))(lambda: straight(k))

    wide = (4, 5, 2, 3) if relayed else (2, 3)

    def send(r, buf, s, ways):
        each(ways, lambda k: halo(buf, s, k).start(), lambda k: detour(r, buf, s, k).start())

    def wait_sent(buf, s):
        each(wide + (0, 1), lambda k: halo(buf, s, k).wait_send(),
             lambda k: detour(0, buf, s, k).wait_send())

    def wait_halo(buf, s):
        for k in wide + (0, 1):
            pl.when(has[pieces[k][0] ^ 1])(lambda: halo(buf, s, k).wait_recv())

    def pass_on(r, s):
        if not relayed:
            return
        for k in (4, 5):
            @pl.when(serves[pieces[k][0]])
            def _():
                buf = r % 2 if isinstance(r, int) else lax.rem(r, 2)
                detour(r, buf, s, k).wait_recv()
                forward(r, buf, s, k).start()

    for s in range(shots):
        load(now_hbm, 0, s, 0).wait()
        send(0, 0, s, wide + (0, 1))

    z_index = place["depth"] * depth + lax.broadcasted_iota(jnp.int32, (depth, width), 0)
    total = depth * sizes["depth"]
    begin = jnp.full((depth, width), start[0], jnp.int32)
    ratio = (z_index - begin + 1).astype(jnp.float32) / (total - begin).astype(jnp.float32)
    damping = jnp.where(z_index >= begin, DAMPING * ratio * ratio, jnp.float32(0.0))
    inverse = 1.0 / (1.0 + damping)
    scale[0] = inverse
    scale[1] = 2.0 * inverse

    load_class.wait()

    def lookup(x, c):
        held = klass[x]
        value = jnp.zeros((depth, width), jnp.float32)
        for k in range(classes):
            value = jnp.where(held == k, courant[k], value)
        speed[x] = value * scale[0]
        return c

    lax.fori_loop(0, rows, lookup, 0)
    for s in range(shots):
        load(before_hbm, 1, s, 1).wait()

    lag = min(LAG, shots)
    for s in range(shots - lag):
        pass_on(0, s)

    lane = lax.broadcasted_iota(jnp.int32, (T, width), 1)
    low = [jnp.where(lane >= k, jnp.float32(COEFFS[k]), 0.0) for k in range(1, W + 1)]
    high = [jnp.where(lane < width - k, jnp.float32(COEFFS[k]), 0.0) for k in range(1, W + 1)]
    x_anchor = place["gx"] * rows

    def compute(t, s, buf, other):
        lane_z = lax.broadcasted_iota(jnp.int32, (depth, width), 1)
        hit = (z_index == cells[s, 1]) & (lane_z == cells[s, 2])
        pulse = jnp.where(hit, wavelet[s, t] * scale[0], 0.0)
        cell_x = cells[s, 0] - x_anchor

        group = math.gcd(rows, GROUP)

        def block_of(x, j):
            z = T + j * T

            def at(dx, dz):
                return grid[buf, s, x + W + dx, pl.ds(z + dz, T), :]

            p = at(0, 0)
            lap = (3.0 * COEFFS[0]) * p
            for k in range(1, W + 1):
                pair = (at(k, 0) + at(-k, 0)) + (at(0, k) + at(0, -k))
                lap = lap + COEFFS[k] * pair
                lap = lap + (
                    low[k - 1] * pltpu.roll(p, k, 1)
                    + high[k - 1] * pltpu.roll(p, width - k, 1)
                )
            q = grid[other, s, x + W, pl.ds(z, T), :]
            block = pl.ds(j * T, T)
            nxt = scale[1, block, :] * (p - q) + q + speed[x, block, :] * lap
            amp = jnp.where(x == cell_x, jnp.float32(1.0), jnp.float32(0.0))
            return nxt + amp * pulse[j * T : (j + 1) * T]

        def row(g, c):
            spots = [(g * group + i, j) for i in range(group) for j in range(depth // T)]
            values = [block_of(x, j) for x, j in spots]
            for (x, j), value in zip(spots, values):
                grid[other, s, x + W, pl.ds(T + j * T, T), :] = value
            return c

        count = rows // group
        edges = min(count, 2)
        lax.fori_loop(0, edges, lambda g, c: row(g * (count - 1), c), 0)

        @pl.when(t < iters - 1)
        def _():
            send(t + 1, other, s, wide)

        lax.fori_loop(1, count - 1, row, 0)

    def step(t, c):
        buf = lax.rem(t, 2)
        other = 1 - buf

        def shot(s, c):
            wait_halo(buf, s)

            @pl.when(t >= 1)
            def _():
                wait_sent(other, s)

            compute(t, s, buf, other)

            @pl.when(t < iters - 1)
            def _():
                send(t + 1, other, s, (0, 1))

            unit = t * shots + s + shots - lag
            r, u = unit // shots, lax.rem(unit, shots)

            @pl.when(r < iters)
            def _():
                pass_on(r, u)

            return c

        return lax.fori_loop(0, shots, shot, c)

    lax.fori_loop(0, iters, step, 0)
    for s in range(shots):
        wait_sent(1 - iters % 2, s)
    if relayed:
        for k in (4, 5):
            @pl.when(serves[pieces[k][0]])
            def _():
                def gone(i, c):
                    r = i // shots
                    forward(r, lax.rem(r, 2), lax.rem(i, shots), k).wait_send()
                    return c
                lax.fori_loop(0, iters * shots, gone, 0)


def put_out(iters, shots, rows, depth, grid, final_hbm, prior_hbm, out_sem):
    xs, zs = pl.ds(W, rows), pl.ds(T, depth)
    copies = [
        pltpu.make_async_copy(grid.at[buf, s, xs, zs, :], out.at[s], out_sem.at[k, s])
        for s in range(shots)
        for k, (buf, out) in enumerate(((iters % 2, final_hbm), (1 - iters % 2, prior_hbm)))
    ]
    for copy in copies:
        copy.start()
    for copy in copies:
        copy.wait()


def solution(mesh):
    sizes = {axis: mesh.shape[axis] for axis in ("depth", "gx")}
    side = math.isqrt(sizes["gx"])
    if side * side != sizes["gx"]:
        side = 0

    def local(now, before, class_map, courant, cells, wavelet, start):
        shots, rows, depth, width = now.shape
        iters = wavelet.shape[0]
        split = side if depth >= 2 * T else 0
        body = functools.partial(
            kernel, sizes, split, iters, shots, rows, depth, width, courant.shape[0]
        )
        whole = pl.BlockSpec(memory_space=pl.ANY)
        far = pl.BlockSpec(memory_space=pltpu.HBM)
        scalar = pl.BlockSpec(memory_space=pltpu.SMEM)
        out = jax.ShapeDtypeStruct(now.shape, jnp.float32)
        half = max(T, depth // 2 // T * T)
        now, before, class_map = (
            pltpu.with_memory_space_constraint(a, pltpu.HBM) for a in (now, before, class_map)
        )
        grid = pl.pallas_call(
            body,
            out_shape=pltpu.VMEM(
                (2, shots, rows + 2 * W, depth + 2 * T, width), jnp.float32
            ),
            in_specs=[far] * 3 + [scalar] * 4,
            out_specs=pl.BlockSpec(memory_space=pltpu.VMEM),
            scratch_shapes=[
                pltpu.VMEM((iters, shots, W, depth - half, width), jnp.float32),
                pltpu.VMEM((rows, depth, width), jnp.float32),
                pltpu.VMEM((2, depth, width), jnp.float32),
                pltpu.VMEM((rows, depth, width), jnp.int32),
                pltpu.SemaphoreType.DMA((2, shots)),
                pltpu.SemaphoreType.DMA,
                pltpu.SemaphoreType.DMA((2, shots, 6)),
                pltpu.SemaphoreType.DMA((2, shots, 6)),
                pltpu.SemaphoreType.DMA((iters, shots)),
                pltpu.SemaphoreType.DMA((iters, shots)),
            ],
            compiler_params=pltpu.CompilerParams(
                collective_id=0, has_side_effects=True, vmem_limit_bytes=16 * 1024 * 1024
            ),
            name="wave",
        )(now, before, class_map, courant, cells, wavelet.T, start)
        grid = pltpu.with_memory_space_constraint(grid, pltpu.VMEM)
        return pl.pallas_call(
            functools.partial(put_out, iters, shots, rows, depth),
            out_shape=(out, out),
            in_specs=[whole],
            out_specs=(whole, whole),
            scratch_shapes=[pltpu.SemaphoreType.DMA((2, shots))],
            compiler_params=pltpu.CompilerParams(vmem_limit_bytes=1024 * 1024),
            name="put_out",
        )(grid)

    placed = P(None, "gx", "depth", None)
    return jax.shard_map(
        local,
        mesh=mesh,
        in_specs=(placed, placed, P("gx", "depth", None), P(), P(), P(), P()),
        out_specs=(placed, placed),
        check_vma=False,
    )
```

time: 106 us -> 83.8 us (0.79)
  Pallas kernels: 98.5 us -> 80.3 us
  local copies, waits for them, and re-layouts: 5.9 us -> 2.01 us
    pallas_call x1 -> x2, Pallas kernels: 98.5 us -> 80.3 us  [the longest x1 78.2 us: local(): pl.pallas_call(body, out_shape=pltpu.VMEM((2, shots, rows + 2 * W, depth...]
    unnamed x5 -> x6, local copies, waits for them, and re-layouts: 5.9 us -> 2.01 us
where the time goes in v1:
time: 83.8 us; the launch traced here: 83.6 us
  Pallas kernels  80.3 us (96%)
  local copies, waits for them, and re-layouts  2.01 us (2%)
  between operations  1.3 us (2%)
    pallas_call x1, Pallas kernels, local(): pl.pallas_call(body, out_shape=pltpu.VMEM((2, shots, rows + 2 * W, depth...  78.2 us
    pallas_call x1, Pallas kernels, local(): pl.pallas_call(functools.partial(put_out, iters, shots, rows, depth), out...  2.07 us
    unnamed x6, local copies, waits for them, and re-layouts  2.01 us

profile of v1, /device:TPU:0, one launch (start us, length us, event | category | flops | bytes accessed | tf_op | source)
XLA Modules:
  0.0 83.6 jit_solution(4198239723936276679)
XLA Ops:
  1.3 0.0 copy-start
  1.3 0.7 copy-done
  2.0 0.0 copy-start.1
  2.0 0.7 copy-done.1
  2.6 0.0 copy-start.2
  2.6 0.7 copy-done.2
  3.3 78.2 %wave.1.grid = f32[2,4,40,48,128]{4,3,2,1,0:T(8,128)S(1)} custom-call(f32[4,32,32,128]{3,2,1,0:T(8,128)} %now_hbm.1, f32[4,32,32,128]{3,2,1,0:T(8,128)} %before_hbm.1, s32[32,32,128]{2,1,0:T(8,128)} %class_hbm.1, f32[8]{0:T(128)S(1)} %copy-done.2, s32[4,3]{1,0:T(4,128)S(1)} %copy-done, f32[4,8]{1,0:T(4,128)S(1)} %bitcast.1, s32[1]{0:T(128)S(6)} %copy.9.start), custom_call_target="tpu_custom_call" | custom-call | tf_op jit(solution)/shard_map/wave/pallas_call | solution.py:341
  81.5 2.1 %put_out.1 = (f32[4,32,32,128]{3,2,1,0:T(8,128)}, f32[4,32,32,128]{3,2,1,0:T(8,128)}) custom-call(f32[2,4,40,48,128]{4,3,2,1,0:T(8,128)S(1)} %wave.1.grid), custom_call_target="tpu_custom_call" | custom-call | tf_op jit(solution)/shard_map/put_out/pallas_call | solution.py:366
Async XLA Ops:
  1.3 0.7 copy-start
  2.0 0.7 copy-start.1
  2.6 0.7 copy-start.2

commit v2 on v1

--- a/solution.py
+++ b/solution.py
@@ -13,15 +13,17 @@
 GROUP = 8
 W = 4
 T = 8
-LAG = 1
+LAG = 2
+ZL = W
 DIRS = (("depth", -1), ("depth", 1), ("gx", -1), ("gx", 1))
 MESH = pl.DeviceIdType.MESH
 
 
 def kernel(
     sizes, side, iters, shots, rows, depth, width, classes,
-    now_hbm, before_hbm, class_hbm, courant, cells, wavelet, start,
+    now_hbm, before_hbm, class_hbm, courant_hbm, cells_hbm, wavelet_hbm, start,
     grid,
+    courant, cells, wavelet, scalar_sem,
     relay, speed, scale, klass, load_sem, class_sem,
     send_sem, recv_sem, relay_sem, forward_sem,
 ):
@@ -65,14 +67,22 @@
 
     for s in range(shots):
         load(now_hbm, 0, s, 0).start()
+    scalars = [
+        pltpu.make_async_copy(a, b, scalar_sem.at[i])
+        for i, (a, b) in enumerate((
+            (courant_hbm, courant), (cells_hbm, cells), (wavelet_hbm, wavelet),
+        ))
+    ]
+    for copy in scalars:
+        copy.start()
     load_class = pltpu.make_async_copy(class_hbm, klass, class_sem)
     load_class.start()
     for s in range(shots):
         load(before_hbm, 1, s, 1).start()
 
     pieces = [
-        (0, xs, pl.ds(T, T), xs, pl.ds(T + depth, T)),
-        (1, xs, pl.ds(depth, T), xs, pl.ds(0, T)),
+        (0, xs, pl.ds(T, ZL), xs, pl.ds(T + depth, ZL)),
+        (1, xs, pl.ds(T + depth - ZL, ZL), xs, pl.ds(T - ZL, ZL)),
         (2, pl.ds(W, W), za, pl.ds(W + rows, W), za),
         (3, pl.ds(rows, W), za, pl.ds(0, W), za),
     ]
@@ -162,12 +172,12 @@
     def send(r, buf, s, ways):
         each(ways, lambda k: halo(buf, s, k).start(), lambda k: detour(r, buf, s, k).start())
 
-    def wait_sent(buf, s):
-        each(wide + (0, 1), lambda k: halo(buf, s, k).wait_send(),
+    def wait_sent(buf, s, ways):
+        each(ways, lambda k: halo(buf, s, k).wait_send(),
              lambda k: detour(0, buf, s, k).wait_send())
 
-    def wait_halo(buf, s):
-        for k in wide + (0, 1):
+    def wait_halo(buf, s, ways):
+        for k in ways:
             pl.when(has[pieces[k][0] ^ 1])(lambda: halo(buf, s, k).wait_recv())
 
     def pass_on(r, s):
@@ -184,6 +194,8 @@
         load(now_hbm, 0, s, 0).wait()
         send(0, 0, s, wide + (0, 1))
 
+    for copy in scalars:
+        copy.wait()
     z_index = place["depth"] * depth + lax.broadcasted_iota(jnp.int32, (depth, width), 0)
     total = depth * sizes["depth"]
     begin = jnp.full((depth, width), start[0], jnp.int32)
@@ -216,13 +228,11 @@
     high = [jnp.where(lane < width - k, jnp.float32(COEFFS[k]), 0.0) for k in range(1, W + 1)]
     x_anchor = place["gx"] * rows
 
-    def compute(t, s, buf, other):
+    def compute(t, s, buf, other, first, group, stride, count):
         lane_z = lax.broadcasted_iota(jnp.int32, (depth, width), 1)
         hit = (z_index == cells[s, 1]) & (lane_z == cells[s, 2])
         pulse = jnp.where(hit, wavelet[s, t] * scale[0], 0.0)
         cell_x = cells[s, 0] - x_anchor
-
-        group = math.gcd(rows, GROUP)
 
         def block_of(x, j):
             z = T + j * T
@@ -246,53 +256,44 @@
             return nxt + amp * pulse[j * T : (j + 1) * T]
 
         def row(g, c):
-            spots = [(g * group + i, j) for i in range(group) for j in range(depth // T)]
+            begin = first + g * stride
+            spots = [(begin + i, j) for i in range(group) for j in range(depth // T)]
             values = [block_of(x, j) for x, j in spots]
             for (x, j), value in zip(spots, values):
                 grid[other, s, x + W, pl.ds(T + j * T, T), :] = value
             return c
 
-        count = rows // group
-        edges = min(count, 2)
-        lax.fori_loop(0, edges, lambda g, c: row(g * (count - 1), c), 0)
-
-        @pl.when(t < iters - 1)
-        def _():
-            send(t + 1, other, s, wide)
-
-        lax.fori_loop(1, count - 1, row, 0)
+        lax.fori_loop(0, count, row, 0)
+
+    inner = rows - 2 * W
+    group = math.gcd(inner, GROUP)
 
     def step(t, c):
         buf = lax.rem(t, 2)
         other = 1 - buf
 
         def shot(s, c):
-            wait_halo(buf, s)
-
-            @pl.when(t >= 1)
-            def _():
-                wait_sent(other, s)
-
-            compute(t, s, buf, other)
+            wait_halo(buf, s, (0, 1))
+            pl.when(t >= 1)(lambda: wait_sent(other, s, (0, 1)))
+            compute(t, s, buf, other, W, group, group, inner // group)
+            wait_halo(buf, s, wide)
+            pl.when(t >= 1)(lambda: wait_sent(other, s, wide))
+            compute(t, s, buf, other, 0, W, rows - W, 2)
 
             @pl.when(t < iters - 1)
             def _():
-                send(t + 1, other, s, (0, 1))
+                send(t + 1, other, s, wide + (0, 1))
 
             unit = t * shots + s + shots - lag
             r, u = unit // shots, lax.rem(unit, shots)
-
-            @pl.when(r < iters)
-            def _():
-                pass_on(r, u)
-
+            pl.when(r < iters)(lambda: pass_on(r, u))
             return c
 
         return lax.fori_loop(0, shots, shot, c)
 
     lax.fori_loop(0, iters, step, 0)
     for s in range(shots):
-        wait_sent(1 - iters % 2, s)
+        wait_sent(1 - iters % 2, s, wide + (0, 1))
     if relayed:
         for k in (4, 5):
             @pl.when(serves[pieces[k][0]])
@@ -332,20 +333,24 @@
         )
         whole = pl.BlockSpec(memory_space=pl.ANY)
         far = pl.BlockSpec(memory_space=pltpu.HBM)
-        scalar = pl.BlockSpec(memory_space=pltpu.SMEM)
         out = jax.ShapeDtypeStruct(now.shape, jnp.float32)
         half = max(T, depth // 2 // T * T)
-        now, before, class_map = (
-            pltpu.with_memory_space_constraint(a, pltpu.HBM) for a in (now, before, class_map)
-        )
+        operands = [
+            pltpu.with_memory_space_constraint(a, pltpu.HBM)
+            for a in (now, before, class_map, courant, cells, wavelet.T)
+        ]
         grid = pl.pallas_call(
             body,
             out_shape=pltpu.VMEM(
                 (2, shots, rows + 2 * W, depth + 2 * T, width), jnp.float32
             ),
-            in_specs=[far] * 3 + [scalar] * 4,
+            in_specs=[far] * len(operands) + [pl.BlockSpec(memory_space=pltpu.SMEM)],
             out_specs=pl.BlockSpec(memory_space=pltpu.VMEM),
             scratch_shapes=[
+                pltpu.SMEM(courant.shape, courant.dtype),
+                pltpu.SMEM(cells.shape, cells.dtype),
+                pltpu.SMEM(wavelet.shape[::-1], wavelet.dtype),
+                pltpu.SemaphoreType.DMA((3,)),
                 pltpu.VMEM((iters, shots, W, depth - half, width), jnp.float32),
                 pltpu.VMEM((rows, depth, width), jnp.float32),
                 pltpu.VMEM((2, depth, width), jnp.float32),
@@ -361,7 +366,7 @@
                 collective_id=0, has_side_effects=True, vmem_limit_bytes=16 * 1024 * 1024
             ),
             name="wave",
-        )(now, before, class_map, courant, cells, wavelet.T, start)
+        )(*operands, start)
         grid = pltpu.with_memory_space_constraint(grid, pltpu.VMEM)
         return pl.pallas_call(
             functools.partial(put_out, iters, shots, rows, depth),

time: 83.8 us -> 80 us (0.955)
  local copies, waits for them, and re-layouts: 2.01 us -> 0 us
  Pallas kernels: 80.3 us -> 78.6 us
    unnamed x6 -> x0, local copies, waits for them, and re-layouts: 2.01 us -> none
    pallas_call x1, Pallas kernels: 78.2 us -> 76.5 us  [local(): pl.pallas_call(body, out_shape=pltpu.VMEM((2, shots, rows + 2 * W, depth...]
where the time goes in v2:
time: 80 us; the launch traced here: 79.9 us
  Pallas kernels  78.6 us (98%)
  between operations  1.29 us (2%)
    pallas_call x1, Pallas kernels, local(): pl.pallas_call(body, out_shape=pltpu.VMEM((2, shots, rows + 2 * W, depth...  76.5 us
    pallas_call x1, Pallas kernels, local(): pl.pallas_call(functools.partial(put_out, iters, shots, rows, depth), out...  2.07 us

profile of v2, /device:TPU:0, one launch (start us, length us, event | category | flops | bytes accessed | tf_op | source)
XLA Modules:
  0.0 79.9 jit_solution(1572581453313318096)
XLA Ops:
  1.3 76.5 %wave.1.grid = f32[2,4,40,48,128]{4,3,2,1,0:T(8,128)S(1)} custom-call(f32[4,32,32,128]{3,2,1,0:T(8,128)} %now_hbm.1, f32[4,32,32,128]{3,2,1,0:T(8,128)} %before_hbm.1, s32[32,32,128]{2,1,0:T(8,128)} %class_hbm.1, f32[8]{0:T(128)} %courant_hbm.1, s32[4,3]{1,0:T(4,128)} %cells_hbm.1, f32[4,8]{1,0:T(4,128)} %bitcast.1, s32[1]{0:T(128)S(6)} %copy.9.start), custom_call_target="tpu_custom_call" | custom-call | tf_op jit(solution)/shard_map/wave/pallas_call | solution.py:342
  77.8 2.1 %put_out.1 = (f32[4,32,32,128]{3,2,1,0:T(8,128)}, f32[4,32,32,128]{3,2,1,0:T(8,128)}) custom-call(f32[2,4,40,48,128]{4,3,2,1,0:T(8,128)S(1)} %wave.1.grid), custom_call_target="tpu_custom_call" | custom-call | tf_op jit(solution)/shard_map/put_out/pallas_call | solution.py:371

commit v3 on v2

--- a/solution.py
+++ b/solution.py
@@ -55,6 +55,23 @@
         serve_from = {2: me + side, 3: me - side}
         serve_to = {2: me + side - 1, 3: me - side + 1}
 
+    meets = [(has[d], target(d)) for d in range(4)]
+    if relayed:
+        for d in (2, 3):
+            step_back = -side + 1 if d == 2 else side - 1
+            back = me - step_back - (1 if d == 2 else -1)
+            meets.append((cross[d], along(via[d])))
+            meets.append((serves[d], along(serve_from[d])))
+            if side > 2:
+                meets.append((serves[d], along(serve_to[d])))
+                meets.append((cross[d], along(me + (side - 1 if d == 2 else 1 - side))))
+
+    barrier = pltpu.get_barrier_semaphore()
+    for there, device in meets:
+        @pl.when(there)
+        def _():
+            pl.semaphore_signal(barrier, inc=1, device_id=device, device_id_type=MESH)
+
     half = max(T, depth // 2 // T * T) if relayed else depth
 
     xs, zs = pl.ds(W, rows), pl.ds(T, depth)
@@ -76,9 +93,6 @@
     for copy in scalars:
         copy.start()
     load_class = pltpu.make_async_copy(class_hbm, klass, class_sem)
-    load_class.start()
-    for s in range(shots):
-        load(before_hbm, 1, s, 1).start()
 
     pieces = [
         (0, xs, pl.ds(T, ZL), xs, pl.ds(T + depth, ZL)),
@@ -90,6 +104,8 @@
         pieces += [
             (2, pl.ds(W, W), zb, pl.ds(W + rows, W), zb),
             (3, pl.ds(rows, W), zb, pl.ds(0, W), zb),
+            (2, pl.ds(W, W), zs, pl.ds(W + rows, W), zs),
+            (3, pl.ds(rows, W), zs, pl.ds(0, W), zs),
         ]
 
     def halo(buf, s, k):
@@ -139,46 +155,52 @@
                     return c
                 lax.fori_loop(0, shots, clear, 0)
 
-    meets = [(has[d], target(d)) for d in range(4)]
-    if relayed:
-        for d in (2, 3):
-            step_back = -side + 1 if d == 2 else side - 1
-            back = me - step_back - (1 if d == 2 else -1)
-            meets.append((cross[d], along(via[d])))
-            meets.append((serves[d], along(serve_from[d])))
-            if side > 2:
-                meets.append((serves[d], along(serve_to[d])))
-                meets.append((cross[d], along(me + (side - 1 if d == 2 else 1 - side))))
-
-    barrier = pltpu.get_barrier_semaphore()
-    for there, device in meets:
-        @pl.when(there)
-        def _():
-            pl.semaphore_signal(barrier, inc=1, device_id=device, device_id_type=MESH)
     peers = sum(there.astype(jnp.int32) for there, _ in meets)
     pl.semaphore_wait(barrier, peers)
 
     def each(ways, straight, around):
-        for k in ways:
-            d = pieces[k][0]
-            if k < 4:
-                pl.when(has[d])(lambda: straight(k))
-            else:
-                pl.when(cross[d])(lambda: around(k))
-                pl.when(has[d] & jnp.logical_not(cross[d]))(lambda: straight(k))
-
-    wide = (4, 5, 2, 3) if relayed else (2, 3)
+        for d in ways:
+            if d < 2 or not relayed:
+                pl.when(has[d])(lambda: straight(d))
+                continue
+
+            @pl.when(cross[d])
+            def _():
+                around(d + 2)
+                straight(d)
+
+            pl.when(has[d] & jnp.logical_not(cross[d]))(lambda: straight(d + 4))
+
+    wide = (2, 3)
 
     def send(r, buf, s, ways):
         each(ways, lambda k: halo(buf, s, k).start(), lambda k: detour(r, buf, s, k).start())
+
+    def send_around(r, buf, s):
+        if relayed:
+            for d in wide:
+                pl.when(cross[d])(lambda: detour(r, buf, s, d + 2).start())
+
+    def send_straight(r, buf, s):
+        each(wide, lambda k: halo(buf, s, k).start(), lambda k: None)
 
     def wait_sent(buf, s, ways):
         each(ways, lambda k: halo(buf, s, k).wait_send(),
              lambda k: detour(0, buf, s, k).wait_send())
 
     def wait_halo(buf, s, ways):
-        for k in ways:
-            pl.when(has[pieces[k][0] ^ 1])(lambda: halo(buf, s, k).wait_recv())
+        for d in ways:
+            if d < 2 or not relayed:
+                pl.when(has[d ^ 1])(lambda: halo(buf, s, d).wait_recv())
+                continue
+
+            @pl.when(cross[d ^ 1])
+            def _():
+                halo(buf, s, d).wait_recv()
+                halo(buf, s, d + 2).wait_recv()
+
+            plain = has[d ^ 1] & jnp.logical_not(cross[d ^ 1])
+            pl.when(plain)(lambda: halo(buf, s, d + 4).wait_recv())
 
     def pass_on(r, s):
         if not relayed:
@@ -190,9 +212,19 @@
                 detour(r, buf, s, k).wait_recv()
                 forward(r, buf, s, k).start()
 
+    lag = min(LAG, shots)
+    early = min(lag, shots)
+    for s in range(early):
+        load(now_hbm, 0, s, 0).wait()
+        send(0, 0, s, wide)
+    for s in range(early, shots):
+        load(now_hbm, 0, s, 0).wait()
+        send_around(0, 0, s)
     for s in range(shots):
-        load(now_hbm, 0, s, 0).wait()
-        send(0, 0, s, wide + (0, 1))
+        send(0, 0, s, (0, 1))
+    load_class.start()
+    for s in range(shots):
+        load(before_hbm, 1, s, 1).start()
 
     for copy in scalars:
         copy.wait()
@@ -219,22 +251,24 @@
     for s in range(shots):
         load(before_hbm, 1, s, 1).wait()
 
-    lag = min(LAG, shots)
-    for s in range(shots - lag):
-        pass_on(0, s)
+    for s in range(early, shots):
+        pass_on(0, s - early)
+        send_straight(0, 0, s)
 
     lane = lax.broadcasted_iota(jnp.int32, (T, width), 1)
     low = [jnp.where(lane >= k, jnp.float32(COEFFS[k]), 0.0) for k in range(1, W + 1)]
     high = [jnp.where(lane < width - k, jnp.float32(COEFFS[k]), 0.0) for k in range(1, W + 1)]
     x_anchor = place["gx"] * rows
 
-    def compute(t, s, buf, other, first, group, stride, count):
+    group = math.gcd(rows, GROUP)
+
+    def compute(t, s, buf, other):
         lane_z = lax.broadcasted_iota(jnp.int32, (depth, width), 1)
         hit = (z_index == cells[s, 1]) & (lane_z == cells[s, 2])
         pulse = jnp.where(hit, wavelet[s, t] * scale[0], 0.0)
         cell_x = cells[s, 0] - x_anchor
 
-        def block_of(x, j):
+        def block_of(x, j, above, below):
             z = T + j * T
 
             def at(dx, dz):
@@ -243,7 +277,11 @@
             p = at(0, 0)
             lap = (3.0 * COEFFS[0]) * p
             for k in range(1, W + 1):
-                pair = (at(k, 0) + at(-k, 0)) + (at(0, k) + at(0, -k))
+                pair = at(0, k) + at(0, -k)
+                if k <= above:
+                    pair = pair + at(-k, 0)
+                if k <= below:
+                    pair = pair + at(k, 0)
                 lap = lap + COEFFS[k] * pair
                 lap = lap + (
                     low[k - 1] * pltpu.roll(p, k, 1)
@@ -255,18 +293,39 @@
             amp = jnp.where(x == cell_x, jnp.float32(1.0), jnp.float32(0.0))
             return nxt + amp * pulse[j * T : (j + 1) * T]
 
+        def run(begin, top, bottom):
+            spots = [(i, j) for i in range(group) for j in range(depth // T)]
+            values = [
+                block_of(begin + i, j, i if top else W, group - 1 - i if bottom else W)
+                for i, j in spots
+            ]
+            for (i, j), value in zip(spots, values):
+                grid[other, s, begin + i + W, pl.ds(T + j * T, T), :] = value
+
+        count = rows // group
+        run(0, True, count == 1)
+        if count > 1:
+            run(rows - group, False, True)
+
         def row(g, c):
-            begin = first + g * stride
-            spots = [(begin + i, j) for i in range(group) for j in range(depth // T)]
-            values = [block_of(x, j) for x, j in spots]
-            for (x, j), value in zip(spots, values):
-                grid[other, s, x + W, pl.ds(T + j * T, T), :] = value
+            run(g * group, False, False)
             return c
 
-        lax.fori_loop(0, count, row, 0)
-
-    inner = rows - 2 * W
-    group = math.gcd(inner, GROUP)
+        lax.fori_loop(1, count - 1, row, 0)
+
+    def complete(s, buf, other):
+        for j in range(depth // T):
+            z = pl.ds(T + j * T, T)
+            block = pl.ds(j * T, T)
+            ahead = [grid[buf, s, W - 1 - k, z, :] for k in range(W)]
+            after = [grid[buf, s, W + rows + k, z, :] for k in range(W)]
+            for i in range(W):
+                for x, beyond in ((i, ahead), (rows - 1 - i, after)):
+                    lap = COEFFS[i + 1] * beyond[0]
+                    for k in range(1, W - i):
+                        lap = lap + COEFFS[i + 1 + k] * beyond[k]
+                    partial = grid[other, s, x + W, z, :]
+                    grid[other, s, x + W, z, :] = partial + speed[x, block, :] * lap
 
     def step(t, c):
         buf = lax.rem(t, 2)
@@ -274,19 +333,20 @@
 
         def shot(s, c):
             wait_halo(buf, s, (0, 1))
-            pl.when(t >= 1)(lambda: wait_sent(other, s, (0, 1)))
-            compute(t, s, buf, other, W, group, group, inner // group)
+            pl.when(t >= 1)(lambda: wait_sent(other, s, (0, 1) + wide))
+            compute(t, s, buf, other)
+
+            unit = t * shots + s + shots - lag
+            r, u = unit // shots, lax.rem(unit, shots)
+            pl.when(r < iters)(lambda: pass_on(r, u))
+
             wait_halo(buf, s, wide)
-            pl.when(t >= 1)(lambda: wait_sent(other, s, wide))
-            compute(t, s, buf, other, 0, W, rows - W, 2)
+            complete(s, buf, other)
 
             @pl.when(t < iters - 1)
             def _():
                 send(t + 1, other, s, wide + (0, 1))
 
-            unit = t * shots + s + shots - lag
-            r, u = unit // shots, lax.rem(unit, shots)
-            pl.when(r < iters)(lambda: pass_on(r, u))
             return c
 
         return lax.fori_loop(0, shots, shot, c)
@@ -357,8 +417,8 @@
                 pltpu.VMEM((rows, depth, width), jnp.int32),
                 pltpu.SemaphoreType.DMA((2, shots)),
                 pltpu.SemaphoreType.DMA,
-                pltpu.SemaphoreType.DMA((2, shots, 6)),
-                pltpu.SemaphoreType.DMA((2, shots, 6)),
+                pltpu.SemaphoreType.DMA((2, shots, 8)),
+                pltpu.SemaphoreType.DMA((2, shots, 8)),
                 pltpu.SemaphoreType.DMA((iters, shots)),
                 pltpu.SemaphoreType.DMA((iters, shots)),
             ],

time: 80 us -> 78.7 us (0.984)
  Pallas kernels: 78.6 us -> 77.3 us
    pallas_call x1, Pallas kernels: 76.5 us -> 75.2 us  [local(): pl.pallas_call(body, out_shape=pltpu.VMEM((2, shots, rows + 2 * W, depth...]
where the time goes in v3:
time: 78.7 us; the launch traced here: 78.6 us
  Pallas kernels  77.3 us (98%)
  between operations  1.29 us (2%)
    pallas_call x1, Pallas kernels, local(): pl.pallas_call(body, out_shape=pltpu.VMEM((2, shots, rows + 2 * W, depth...  75.2 us
    pallas_call x1, Pallas kernels, local(): pl.pallas_call(functools.partial(put_out, iters, shots, rows, depth), out...  2.07 us

profile of v3, /device:TPU:0, one launch (start us, length us, event | category | flops | bytes accessed | tf_op | source)
XLA Modules:
  0.0 78.6 jit_solution(456757170978967148)
XLA Ops:
  1.3 75.2 %wave.1.grid = f32[2,4,40,48,128]{4,3,2,1,0:T(8,128)S(1)} custom-call(f32[4,32,32,128]{3,2,1,0:T(8,128)} %now_hbm.1, f32[4,32,32,128]{3,2,1,0:T(8,128)} %before_hbm.1, s32[32,32,128]{2,1,0:T(8,128)} %class_hbm.1, f32[8]{0:T(128)} %courant_hbm.1, s32[4,3]{1,0:T(4,128)} %cells_hbm.1, f32[4,8]{1,0:T(4,128)} %bitcast.1, s32[1]{0:T(128)S(6)} %copy.9.start), custom_call_target="tpu_custom_call" | custom-call | tf_op jit(solution)/shard_map/wave/pallas_call | solution.py:402
  76.5 2.1 %put_out.1 = (f32[4,32,32,128]{3,2,1,0:T(8,128)}, f32[4,32,32,128]{3,2,1,0:T(8,128)}) custom-call(f32[2,4,40,48,128]{4,3,2,1,0:T(8,128)S(1)} %wave.1.grid), custom_call_target="tpu_custom_call" | custom-call | tf_op jit(solution)/shard_map/put_out/pallas_call | solution.py:431

commit v4 on v3

--- a/solution.py
+++ b/solution.py
@@ -82,6 +82,11 @@
             source.at[s], grid.at[buf, s, xs, zs, :], load_sem.at[k, s]
         )
 
+    def passed(r, s):
+        if relayed:
+            for d in wide:
+                pl.when(serves[d] & bends(r, s))(lambda: forward(r, lax.rem(r, 2), s, d + 2).wait_send())
+
     for s in range(shots):
         load(now_hbm, 0, s, 0).start()
     scalars = [
@@ -158,23 +163,28 @@
     peers = sum(there.astype(jnp.int32) for there, _ in meets)
     pl.semaphore_wait(barrier, peers)
 
-    def each(ways, straight, around):
+    def bends(r, s):
+        last = (r == iters - 1) & (s == shots - 1)
+        return jnp.logical_not(last)
+
+    def each(ways, straight, around, bend=True):
         for d in ways:
             if d < 2 or not relayed:
                 pl.when(has[d])(lambda: straight(d))
                 continue
 
-            @pl.when(cross[d])
+            @pl.when(cross[d] & bend)
             def _():
                 around(d + 2)
                 straight(d)
 
-            pl.when(has[d] & jnp.logical_not(cross[d]))(lambda: straight(d + 4))
+            pl.when(has[d] & jnp.logical_not(cross[d] & bend))(lambda: straight(d + 4))
 
     wide = (2, 3)
 
     def send(r, buf, s, ways):
-        each(ways, lambda k: halo(buf, s, k).start(), lambda k: detour(r, buf, s, k).start())
+        each(ways, lambda k: halo(buf, s, k).start(), lambda k: detour(r, buf, s, k).start(),
+             bends(r, s))
 
     def send_around(r, buf, s):
         if relayed:
@@ -184,29 +194,31 @@
     def send_straight(r, buf, s):
         each(wide, lambda k: halo(buf, s, k).start(), lambda k: None)
 
-    def wait_sent(buf, s, ways):
+    def wait_sent(r, buf, s, ways):
         each(ways, lambda k: halo(buf, s, k).wait_send(),
-             lambda k: detour(0, buf, s, k).wait_send())
-
-    def wait_halo(buf, s, ways):
+             lambda k: detour(0, buf, s, k).wait_send(), bends(r, s))
+
+    def wait_halo(r, buf, s, ways):
         for d in ways:
             if d < 2 or not relayed:
                 pl.when(has[d ^ 1])(lambda: halo(buf, s, d).wait_recv())
                 continue
 
-            @pl.when(cross[d ^ 1])
+            bend = bends(r, s)
+
+            @pl.when(cross[d ^ 1] & bend)
             def _():
                 halo(buf, s, d).wait_recv()
                 halo(buf, s, d + 2).wait_recv()
 
-            plain = has[d ^ 1] & jnp.logical_not(cross[d ^ 1])
+            plain = has[d ^ 1] & jnp.logical_not(cross[d ^ 1] & bend)
             pl.when(plain)(lambda: halo(buf, s, d + 4).wait_recv())
 
     def pass_on(r, s):
         if not relayed:
             return
         for k in (4, 5):
-            @pl.when(serves[pieces[k][0]])
+            @pl.when(serves[pieces[k][0]] & bends(r, s))
             def _():
                 buf = r % 2 if isinstance(r, int) else lax.rem(r, 2)
                 detour(r, buf, s, k).wait_recv()
@@ -332,15 +344,16 @@
         other = 1 - buf
 
         def shot(s, c):
-            wait_halo(buf, s, (0, 1))
-            pl.when(t >= 1)(lambda: wait_sent(other, s, (0, 1) + wide))
+            wait_halo(t, buf, s, (0, 1))
             compute(t, s, buf, other)
+            wait_sent(t, buf, s, (0, 1) + wide)
+            passed(t, s)
 
             unit = t * shots + s + shots - lag
             r, u = unit // shots, lax.rem(unit, shots)
             pl.when(r < iters)(lambda: pass_on(r, u))
 
-            wait_halo(buf, s, wide)
+            wait_halo(t, buf, s, wide)
             complete(s, buf, other)
 
             @pl.when(t < iters - 1)
@@ -352,17 +365,6 @@
         return lax.fori_loop(0, shots, shot, c)
 
     lax.fori_loop(0, iters, step, 0)
-    for s in range(shots):
-        wait_sent(1 - iters % 2, s, wide + (0, 1))
-    if relayed:
-        for k in (4, 5):
-            @pl.when(serves[pieces[k][0]])
-            def _():
-                def gone(i, c):
-                    r = i // shots
-                    forward(r, lax.rem(r, 2), lax.rem(i, shots), k).wait_send()
-                    return c
-                lax.fori_loop(0, iters * shots, gone, 0)
 
 
 def put_out(iters, shots, rows, depth, grid, final_hbm, prior_hbm, out_sem):

time: 78.7 us -> 78.2 us (level)
  no operation moved by 1% of the time
where the time goes in v4:
time: 78.2 us; the launch traced here: 78 us
  Pallas kernels  76.8 us (98%)
  between operations  1.29 us (2%)
    pallas_call x1, Pallas kernels, local(): pl.pallas_call(body, out_shape=pltpu.VMEM((2, shots, rows + 2 * W, depth...  74.7 us
    pallas_call x1, Pallas kernels, local(): pl.pallas_call(functools.partial(put_out, iters, shots, rows, depth), out...  2.07 us

profile of v4, /device:TPU:0, one launch (start us, length us, event | category | flops | bytes accessed | tf_op | source)
XLA Modules:
  0.0 78.0 jit_solution(8223804419774714474)
XLA Ops:
  1.3 74.7 %wave.1.grid = f32[2,4,40,48,128]{4,3,2,1,0:T(8,128)S(1)} custom-call(f32[4,32,32,128]{3,2,1,0:T(8,128)} %now_hbm.1, f32[4,32,32,128]{3,2,1,0:T(8,128)} %before_hbm.1, s32[32,32,128]{2,1,0:T(8,128)} %class_hbm.1, f32[8]{0:T(128)} %courant_hbm.1, s32[4,3]{1,0:T(4,128)} %cells_hbm.1, f32[4,8]{1,0:T(4,128)} %bitcast.1, s32[1]{0:T(128)S(6)} %copy.9.start), custom_call_target="tpu_custom_call" | custom-call | tf_op jit(solution)/shard_map/wave/pallas_call | solution.py:404
  76.0 2.1 %put_out.1 = (f32[4,32,32,128]{3,2,1,0:T(8,128)}, f32[4,32,32,128]{3,2,1,0:T(8,128)}) custom-call(f32[2,4,40,48,128]{4,3,2,1,0:T(8,128)S(1)} %wave.1.grid), custom_call_target="tpu_custom_call" | custom-call | tf_op jit(solution)/shard_map/put_out/pallas_call | solution.py:433

commit v5 on v4

--- a/solution.py
+++ b/solution.py
@@ -21,9 +21,9 @@
 
 def kernel(
     sizes, side, iters, shots, rows, depth, width, classes,
-    now_hbm, before_hbm, class_hbm, courant_hbm, cells_hbm, wavelet_hbm, start,
+    now_hbm, before_hbm, class_hbm, courant_hbm, cells_hbm, wavelet_hbm, start_hbm,
     grid,
-    courant, cells, wavelet, scalar_sem,
+    courant, cells, wavelet, start, scalar_sem,
     relay, speed, scale, klass, load_sem, class_sem,
     send_sem, recv_sem, relay_sem, forward_sem,
 ):
@@ -93,6 +93,7 @@
         pltpu.make_async_copy(a, b, scalar_sem.at[i])
         for i, (a, b) in enumerate((
             (courant_hbm, courant), (cells_hbm, cells), (wavelet_hbm, wavelet),
+            (start_hbm, start),
         ))
     ]
     for copy in scalars:
@@ -242,7 +243,7 @@
         copy.wait()
     z_index = place["depth"] * depth + lax.broadcasted_iota(jnp.int32, (depth, width), 0)
     total = depth * sizes["depth"]
-    begin = jnp.full((depth, width), start[0], jnp.int32)
+    begin = jnp.full((depth, width), start[0, 0], jnp.int32)
     ratio = (z_index - begin + 1).astype(jnp.float32) / (total - begin).astype(jnp.float32)
     damping = jnp.where(z_index >= begin, DAMPING * ratio * ratio, jnp.float32(0.0))
     inverse = 1.0 / (1.0 + damping)
@@ -406,13 +407,14 @@
             out_shape=pltpu.VMEM(
                 (2, shots, rows + 2 * W, depth + 2 * T, width), jnp.float32
             ),
-            in_specs=[far] * len(operands) + [pl.BlockSpec(memory_space=pltpu.SMEM)],
+            in_specs=[far] * len(operands) + [whole],
             out_specs=pl.BlockSpec(memory_space=pltpu.VMEM),
             scratch_shapes=[
                 pltpu.SMEM(courant.shape, courant.dtype),
                 pltpu.SMEM(cells.shape, cells.dtype),
                 pltpu.SMEM(wavelet.shape[::-1], wavelet.dtype),
-                pltpu.SemaphoreType.DMA((3,)),
+                pltpu.SMEM((1, 1), start.dtype),
+                pltpu.SemaphoreType.DMA((4,)),
                 pltpu.VMEM((iters, shots, W, depth - half, width), jnp.float32),
                 pltpu.VMEM((rows, depth, width), jnp.float32),
                 pltpu.VMEM((2, depth, width), jnp.float32),
@@ -428,7 +430,7 @@
                 collective_id=0, has_side_effects=True, vmem_limit_bytes=16 * 1024 * 1024
             ),
             name="wave",
-        )(*operands, start)
+        )(*operands, start.reshape(1, 1))
         grid = pltpu.with_memory_space_constraint(grid, pltpu.VMEM)
         return pl.pallas_call(
             functools.partial(put_out, iters, shots, rows, depth),

time: 78.2 us -> 78.2 us (level)
  no operation moved by 1% of the time
where the time goes in v5:
time: 78.2 us; the launch traced here: 78 us
  Pallas kernels  76.8 us (98%)
  between operations  1.29 us (2%)
    pallas_call x1, Pallas kernels, local(): pl.pallas_call(body, out_shape=pltpu.VMEM((2, shots, rows + 2 * W, depth...  74.7 us
    pallas_call x1, Pallas kernels, local(): pl.pallas_call(functools.partial(put_out, iters, shots, rows, depth), out...  2.07 us

profile of v5, /device:TPU:0, one launch (start us, length us, event | category | flops | bytes accessed | tf_op | source)
XLA Modules:
  0.0 78.0 jit_solution(8503058883638440470)
XLA Ops:
  1.3 74.7 %wave.1.grid = f32[2,4,40,48,128]{4,3,2,1,0:T(8,128)S(1)} custom-call(f32[4,32,32,128]{3,2,1,0:T(8,128)} %now_hbm.1, f32[4,32,32,128]{3,2,1,0:T(8,128)} %before_hbm.1, s32[32,32,128]{2,1,0:T(8,128)} %class_hbm.1, f32[8]{0:T(128)} %courant_hbm.1, s32[4,3]{1,0:T(4,128)} %cells_hbm.1, f32[4,8]{1,0:T(4,128)} %bitcast.3, s32[1,1]{1,0:T(1,128)} %bitcast.2.start_hbm), custom_call_target="tpu_custom_call" | custom-call | tf_op jit(solution)/shard_map/wave/pallas_call | solution.py:405
  76.0 2.1 %put_out.1 = (f32[4,32,32,128]{3,2,1,0:T(8,128)}, f32[4,32,32,128]{3,2,1,0:T(8,128)}) custom-call(f32[2,4,40,48,128]{4,3,2,1,0:T(8,128)S(1)} %wave.1.grid), custom_call_target="tpu_custom_call" | custom-call | tf_op jit(solution)/shard_map/put_out/pallas_call | solution.py:435
